TPU v7x, 32 devices: a whole 2x2x4 slice. The times are simulated.
32 devices in a mesh: dp: 8 (over z, core), seq: 4 (over y, x).
Axes of the slice: x: 2, y: 2, z: 4, core: 2. Of those that a mesh axis runs over, the one named last changes fastest.
Arguments:
- tokens: bfloat16 [32, 256, 1024], P(('dp', 'seq')), may hold values from -6 to 6
- queries: bfloat16 [32, 256, 1024], P(('dp', 'seq')), may hold values from -240 to 240
- keys: bfloat16 [32, 256, 1024], P(('dp', 'seq')), may hold values from -7 to 7
- values: bfloat16 [32, 256, 1024], P(('dp', 'seq')), may hold values from -6 to 6
- ln_gain: bfloat16 [1024], replicated, may hold values from 0.5 to 1.5
- mean_in: bfloat16 [1024, 2048], P(None, 'seq'), may hold values from -0.1875 to 0.1875
- sigma_in: bfloat16 [1024, 2048], P(None, 'seq'), may hold values from 0.0039978027 to 0.029907227
- noise_in: bfloat16 [1024, 2048], P(None, 'seq'), may hold values from -4 to 4
- mean_out: bfloat16 [2048, 1024], P('seq'), may hold values from -0.125 to 0.125
- sigma_out: bfloat16 [2048, 1024], P('seq'), may hold values from 0.0019989014 to 0.014953613
- noise_out: bfloat16 [2048, 1024], P('seq'), may hold values from -4 to 4
- flip_in: int32 [32, 1024], P('dp'), may hold values from -1 to 1, as said below
- flip_mid: int32 [32, 2048], P('dp', 'seq'), may hold values from -1 to 1, as said below
- flip_hidden: int32 [32, 2048], P('dp', 'seq'), may hold values from -1 to 1, as said below
- flip_out: int32 [32, 1024], P('dp'), may hold values from -1 to 1, as said below
- cotangent: bfloat16 [32, 256, 1024], P(('dp', 'seq')), may hold values from -0.75 to 0.75
Outputs:
- block_out: bfloat16 [32, 256, 1024], P(('dp', 'seq'))
- resid_grad: bfloat16 [32, 256, 1024], P(('dp', 'seq'))
- grad_mean_in: float32 [1024, 2048], P(None, 'seq')
- grad_sigma_in: float32 [1024, 2048], P(None, 'seq')
- grad_mean_out: float32 [2048, 1024], P('seq')
- grad_sigma_out: float32 [2048, 1024], P('seq')
Inputs may be any that keep to these rules, and one draw needn't show every extreme that they name: `flip_in`: each entry is -1 or +1. `flip_mid`: each entry is -1 or +1. `flip_hidden`: each entry is -1 or +1. `flip_out`: each entry is -1 or +1.
All inputs are finite; a program needn't handle non-finite values.
Results may differ from a plain program's by a relative error of at most 0.018.
Values may be sent and summed in bfloat16 or wider, within the bound.
A program may use at most 128 MiB of HBM per device.

v0:
```python
import jax
import jax.numpy as jnp
from jax import lax
from jax.sharding import PartitionSpec as P

HEADS = 16


def gelu_slope(pre):
    cdf = 0.5 * (1.0 + lax.erf(pre * 0.7071067811865476))
    pdf = jnp.exp(-0.5 * pre * pre) * 0.3989422804014327
    return cdf + pre * pdf


def contract_first(left, right):
    return lax.dot_general(
        left, right, (((0,), (0,)), ((), ())), preferred_element_type=jnp.float32
    )


def contract_last(left, right):
    return lax.dot_general(
        left, right, (((1,), (1,)), ((), ())), preferred_element_type=jnp.float32
    )


def body(
    tokens,
    queries,
    keys,
    values,
    ln_gain,
    mean_in,
    sigma_in,
    noise_in,
    mean_out,
    sigma_out,
    noise_out,
    flip_in,
    flip_mid,
    flip_hidden,
    flip_out,
    cotangent,
):
    bf = jnp.bfloat16
    f32 = jnp.float32
    own_images, patches, width = tokens.shape
    hidden_local = mean_in.shape[1]
    head_dim = width // HEADS
    scale = head_dim ** (-0.5)
    pert_in = (sigma_in.astype(f32) * noise_in.astype(f32)).astype(bf)
    pert_out = (sigma_out.astype(f32) * noise_out.astype(f32)).astype(bf)
    query_heads = queries.reshape(own_images, patches, HEADS, head_dim)
    key_heads = keys.reshape(own_images, patches, HEADS, head_dim)
    value_heads = values.reshape(own_images, patches, HEADS, head_dim)
    scores = (
        jnp.einsum("bqhe,bkhe->bhqk", query_heads, key_heads, preferred_element_type=f32) * scale
    )
    top = jnp.max(scores, axis=-1, keepdims=True)
    expd = jnp.exp(scores - top)
    total = jnp.sum(expd, axis=-1)
    accum = jnp.einsum("bhqk,bkhe->bqhe", expd.astype(bf), value_heads, preferred_element_type=f32)
    attn_out = (
        (accum / jnp.transpose(total, (0, 2, 1))[..., None])
        .reshape(own_images, patches, width)
        .astype(bf)
    )
    resid = (tokens.astype(f32) + attn_out.astype(f32)).astype(bf)
    resid_f = resid.astype(f32)
    centered = resid_f - jnp.mean(resid_f, axis=-1, keepdims=True)
    rstd = lax.rsqrt(jnp.mean(centered * centered, axis=-1, keepdims=True) + 1e-06)
    ahat = centered * rstd
    gain_f = ln_gain.astype(f32)
    normed = (ahat * gain_f).astype(bf)
    in_signs = flip_in.astype(bf)[:, None, :]
    in_signs_f = flip_in.astype(f32)[:, None, :]
    mid_signs = flip_mid.astype(bf)[:, None, :]
    mid_signs_f = flip_mid.astype(f32)[:, None, :]
    hid_signs = flip_hidden.astype(bf)[:, None, :]
    hid_signs_f = flip_hidden.astype(f32)[:, None, :]
    out_signs = flip_out.astype(bf)[:, None, :]
    out_signs_f = flip_out.astype(f32)[:, None, :]
    gathered = lax.all_gather(normed, "seq", axis=0, tiled=True)
    count = gathered.shape[0]
    signs = in_signs
    flat = gathered.reshape(-1, width)
    flat_flip = (gathered * signs).reshape(-1, width)
    plain = jnp.dot(flat, mean_in, preferred_element_type=f32).reshape(count, patches, hidden_local)
    noisy = jnp.dot(flat_flip, pert_in, preferred_element_type=f32).reshape(
        count, patches, hidden_local
    )
    pre = plain + noisy * mid_signs_f
    group_images = pre.shape[0]
    rows = group_images * patches
    hidden = jax.nn.gelu(pre, approximate=False).astype(bf)
    flipped_hidden = hidden * hid_signs
    count = lax.axis_size("seq") * own_images
    hb = hidden.reshape(-1, hidden_local)
    hfb = flipped_hidden.reshape(-1, hidden_local)
    plain = jnp.dot(hb, mean_out, preferred_element_type=f32).reshape(count, patches, width)
    noisy = jnp.dot(hfb, pert_out, preferred_element_type=f32).reshape(count, patches, width)
    mixed = lax.psum_scatter(
        (plain + noisy * out_signs_f).astype(jnp.bfloat16), "seq", scatter_dimension=0, tiled=True
    ).astype(jnp.float32)
    block_out = (resid_f + mixed).astype(bf)
    cot_all = lax.all_gather(cotangent, "seq", axis=0, tiled=True)
    cot_flat = cot_all.reshape(rows, width)
    cot_flip_flat = (cot_all * out_signs).reshape(rows, width)
    dhidden = contract_last(cot_flat, mean_out).reshape(group_images, patches, hidden_local)
    dhidden = (
        dhidden
        + contract_last(cot_flip_flat, pert_out).reshape(group_images, patches, hidden_local)
        * hid_signs_f
    )
    dpre = (dhidden * gelu_slope(pre)).astype(bf)
    dpre_flip = dpre * mid_signs
    local_mean_out = contract_first(hidden.reshape(rows, hidden_local), cot_flat)
    local_sigma_out = contract_first(
        flipped_hidden.reshape(rows, hidden_local), cot_flip_flat
    ) * noise_out.astype(f32)
    grad_mean_out, grad_sigma_out = (
        lax.psum(local_mean_out.astype(jnp.bfloat16), "dp").astype(jnp.float32),
        lax.psum(local_sigma_out.astype(jnp.bfloat16), "dp").astype(jnp.float32),
    )
    local_mean_in = contract_first(gathered.reshape(rows, width), dpre.reshape(rows, hidden_local))
    local_flip_in = contract_first(
        (gathered * in_signs).reshape(rows, width), dpre_flip.reshape(rows, hidden_local)
    )
    local_sigma_in = local_flip_in * noise_in.astype(f32)
    count = lax.axis_size("seq") * own_images
    drows = dpre.reshape(-1, hidden_local)
    dflip_rows = dpre_flip.reshape(-1, hidden_local)
    signs = in_signs_f
    plain = contract_last(drows, mean_in).reshape(count, patches, width)
    noisy = contract_last(dflip_rows, pert_in).reshape(count, patches, width)
    dnormed = lax.psum_scatter(
        (plain + noisy * signs).astype(jnp.bfloat16), "seq", scatter_dimension=0, tiled=True
    ).astype(jnp.float32)
    grad_mean_in, grad_sigma_in = (
        lax.psum(local_mean_in.astype(jnp.bfloat16), "dp").astype(jnp.float32),
        lax.psum(local_sigma_in.astype(jnp.bfloat16), "dp").astype(jnp.float32),
    )
    scaled = dnormed * gain_f
    back = rstd * (
        scaled
        - jnp.mean(scaled, axis=-1, keepdims=True)
        - ahat * jnp.mean(scaled * ahat, axis=-1, keepdims=True)
    )
    resid_grad = (cotangent.astype(f32) + back).astype(bf)
    return (block_out, resid_grad, grad_mean_in, grad_sigma_in, grad_mean_out, grad_sigma_out)


def solution(mesh):
    return jax.shard_map(
        body,
        mesh=mesh,
        in_specs=(
            P(("dp", "seq"), None, None),
            P(("dp", "seq"), None, None),
            P(("dp", "seq"), None, None),
            P(("dp", "seq"), None, None),
            P(),
            P(None, "seq"),
            P(None, "seq"),
            P(None, "seq"),
            P("seq", None),
            P("seq", None),
            P("seq", None),
            P("dp", None),
            P("dp", "seq"),
            P("dp", "seq"),
            P("dp", None),
            P(("dp", "seq"), None, None),
        ),
        out_specs=(
            P(("dp", "seq"), None, None),
            P(("dp", "seq"), None, None),
            P(None, "seq"),
            P(None, "seq"),
            P("seq", None),
            P("seq", None),
        ),
        check_vma=False,
    )
```

profile of v0, /device:TPU:0, one launch (start us, length us, event | category | flops | bytes accessed | tf_op | source)
XLA Modules:
  0.0 289.0 jit_solution(1723222755347720097)
XLA Ops:
  7.2 0.0 copy-start
  7.2 0.0 all-gather.3.cloned.1.call-start
  7.2 1.4 copy.42
  8.6 1.2 copy.40
  9.9 0.2 copy.41
  10.1 0.8 multiply_reduce_fusion
  10.8 0.7 fusion
  11.6 0.9 divide_convert_fusion
  12.5 0.1 bitcast_convert_fusion.2
  12.6 1.3 copy.44
  13.9 1.5 convert_reduce_fusion
  15.5 0.3 fusion.51
  15.8 1.1 fusion.45
  16.9 0.0 all-gather.3.cloned.1.call-update
  16.9 0.0 all-gather.5.cloned.1.call-start
  16.9 0.7 all-gather.5.cloned.1.call-update
  17.6 0.2 all-reduce.5.cloned.1.call-start
  18.0 37.0 %all-gather.3.cloned.1.call-done = bf16[4,256,1024]{2,1,0:T(8,128)(2,1)} async-done(((bf16[1,256,1024]{2,1,0:T(8,128)(2,1)}), bf16[4,256,1024]{2,1,0:T(8,128)(2,1)}) %all-gather.3.cloned.1.call-update) | async-done | bytes 2097168 | tf_op jit(solution)/shard_map/all_gather | solution.py:83
  55.0 3.3 %fusion.31 = f32[4,256,512]{2,1,0:T(8,128)S(1)} fusion(bf16[4,256,1024]{2,1,0:T(8,128)(2,1)} %all-gather.3.cloned.1.call-done, bf16[4,1024]{1,0:T(4,128)(2,1)S(1)} %get-tuple-element.19, bf16[1024,512]{1,0:T(8,128)(2,1)S(1)} %copy-done.7, bf16[1024,512]{1,0:T(8,128)(2,1)} %param.22), kind=kOutput, calls=%fused_computation.55 | convolution fusion | flops 1076887552 | bytes 6299648 | tf_op jit(solution)/shard_map/dot_general | solution.py:89
  58.3 1.9 fusion.77
  60.2 1.3 copy-done.4
  61.5 4.7 %fusion.8 = bf16[4,256,512]{2,1,0:T(8,128)(2,1)S(1)} fusion(f32[4,256,512]{2,1,0:T(8,128)S(1)} %get-tuple-element.28, u8[256,512]{1,0:T(8,128)(4,1)S(1)} %get-tuple-element.7, u8[256,512]{1,0:T(8,128)(4,1)S(1)} %get-tuple-element.6), kind=kLoop, calls=%fused_computation.18 | loop fusion | flops 36700160 | bytes 3407872 | tf_op jit(solution)/shard_map/convert_element_type | solution.py:95
  66.2 25.8 %all-gather.5.cloned.1.call-done = bf16[4,256,1024]{2,1,0:T(8,128)(2,1)} async-done(((bf16[1,256,1024]{2,1,0:T(8,128)(2,1)}), bf16[4,256,1024]{2,1,0:T(8,128)(2,1)}) %all-gather.5.cloned.1.call-update) | async-done | bytes 2097168 | tf_op jit(solution)/shard_map/all_gather | solution.py:106
  92.0 3.6 %fusion.27 = f32[4,256,512]{2,1,0:T(8,128)S(1)} fusion(bf16[4,256,1024]{2,1,0:T(8,128)(2,1)} %all-gather.5.cloned.1.call-done, bf16[4,1024]{1,0:T(4,128)(2,1)S(1)} %get-tuple-element.20, bf16[512,1024]{1,0:T(8,128)(2,1)} %param.26, bf16[512,1024]{1,0:T(8,128)(2,1)} %param.25), kind=kOutput, calls=%fused_computation.51 | convolution fusion | flops 1076887552 | bytes 6299648 | tf_op jit(solution)/shard_map/dot_general | solution.py:22
  95.7 0.1 copy-done.17
  95.8 2.0 fusion.14
  97.8 2.3 bitcast_convert_fusion.1
  100.1 2.3 fusion.3
  102.4 2.3 bitcast_convert_fusion
  104.6 2.4 fusion.5
  107.0 0.0 all-reduce.5.cloned.1.call-update
  107.0 0.3 reduce-scatter.9.cloned.1.call-start
  107.3 2.7 fusion.58
  110.0 2.6 add_convert_fusion
  112.6 0.0 reduce-scatter.9.cloned.1.call-update
  112.7 0.0 reduce-scatter.7.cloned.1.call-start
  112.7 2.6 fusion.56
  115.4 2.6 add_convert_fusion.1
  118.0 0.0 reduce-scatter.7.cloned.1.call-update
  118.0 85.7 %all-reduce.5.cloned.1.call-done = (bf16[1024,512]{1,0:T(8,128)(2,1)}, bf16[1024,512]{1,0:T(8,128)(2,1)}, bf16[512,1024]{1,0:T(8,128)(2,1)}, bf16[512,1024]{1,0:T(8,128)(2,1)}) async-done(((bf16[1024,512]{1,0:T(8,128)(2,1)}, bf16[1024,512]{1,0:T(8,128)(2,1)}, bf16[512,1024]{1,0:T(8,128)(2,1)}, bf16[512,1024]{1,0:T(8,128)(2,1)}), (bf16[1024,512]{1,0:T(8,128)(2,1)}, bf16[1024,512]{1,0:T(8,128)(2,1)}, ...) | async-done | bytes 4194320 | tf_op jit(solution)/shard_map/psum | solution.py:140
  203.7 2.9 %convert_element_type.173 = f32[1024,512]{1,0:T(8,128)} convert(bf16[1024,512]{1,0:T(8,128)(2,1)} %get-tuple-element.10) | non-fusion elementwise | flops 524288 | bytes 3145728 | tf_op jit(solution)/shard_map/convert_element_type | solution.py:140
  206.7 1.6 convert_element_type.175
  208.3 1.6 convert_element_type.177
  209.8 1.6 convert_element_type.179
  211.4 30.4 %reduce-scatter.9.cloned.1.call-done = bf16[1,256,1024]{2,1,0:T(8,128)(2,1)} async-done(((bf16[4,256,1024]{2,1,0:T(8,128)(2,1)}), bf16[1,256,1024]{2,1,0:T(8,128)(2,1)}) %reduce-scatter.9.cloned.1.call-update) | async-done | bytes 524304
  241.8 1.4 fusion.61
  243.2 36.6 %reduce-scatter.7.cloned.1.call-done = bf16[1,256,1024]{2,1,0:T(8,128)(2,1)} async-done(((bf16[4,256,1024]{2,1,0:T(8,128)(2,1)}), bf16[1,256,1024]{2,1,0:T(8,128)(2,1)}) %reduce-scatter.7.cloned.1.call-update) | async-done | bytes 524304
  279.8 2.6 fusion.50
  (59 shorter events, 0.2 us)
Async XLA Ops:
  7.2 51.1 %copy-start = (bf16[1024,512]{1,0:T(8,128)(2,1)S(1)}, bf16[1024,512]{1,0:T(8,128)(2,1)}, u32[]{:S(2)}) copy-start(bf16[1024,512]{1,0:T(8,128)(2,1)} %param.21) | copy-start | bytes 3145732
  7.2 2.7 copy-start.18
  7.2 47.8 %all-gather.3.cloned.1.call-start = ((), (), s32[]{:S(2)}) async-start(), calls=%async_computation.2 | async-start | bytes 2621440 | tf_op jit(solution)/shard_map/all_gather | solution.py:83
  12.4 1.4 copy-start.24
  12.4 1.4 copy-start.19
  13.9 4.0 %copy-start.22 = (s32[4,512]{1,0:T(4,128)S(1)}, s32[4,512]{1,0:T(4,128)}, u32[]{:S(2)}) copy-start(s32[4,512]{1,0:T(4,128)} %param.28) | copy-start | bytes 24580
  13.9 4.0 %copy-start.23 = (s32[4,512]{1,0:T(4,128)S(1)}, s32[4,512]{1,0:T(4,128)}, u32[]{:S(2)}) copy-start(s32[4,512]{1,0:T(4,128)} %param.29) | copy-start | bytes 24580
  13.9 4.0 %copy-start.20 = (s32[4,1024]{1,0:T(4,128)S(1)}, s32[4,1024]{1,0:T(4,128)}, u32[]{:S(2)}) copy-start(s32[4,1024]{1,0:T(4,128)} %param.27) | copy-start | bytes 49156
  13.9 4.0 %copy-start.21 = (s32[4,1024]{1,0:T(4,128)S(1)}, s32[4,1024]{1,0:T(4,128)}, u32[]{:S(2)}) copy-start(s32[4,1024]{1,0:T(4,128)} %param.30) | copy-start | bytes 49156
  13.9 41.0 %copy-start.7 = (bf16[1024,512]{1,0:T(8,128)(2,1)S(1)}, bf16[1024,512]{1,0:T(8,128)(2,1)}, u32[]{:S(2)}) copy-start(bf16[1024,512]{1,0:T(8,128)(2,1)} %param.23) | copy-start | bytes 3145732
  16.9 75.1 %all-gather.5.cloned.1.call-start = ((), (), s32[]{:S(2)}) async-start(), calls=%async_computation.3 | async-start | bytes 2621440 | tf_op jit(solution)/shard_map/all_gather | solution.py:106
  17.6 186.1 %all-reduce.5.cloned.1.call-start = ((), (), s32[]{:S(2)}) async-start(), calls=%async_computation.6 | async-start | bytes 8388608 | tf_op jit(solution)/shard_map/psum | solution.py:140
  55.0 3.3 %copy-start.25 = (bf16[4,256,1024]{2,1,0:T(8,128)(2,1)S(1)}, bf16[4,256,1024]{2,1,0:T(8,128)(2,1)}, u32[]{:S(2)}) copy-start(bf16[4,256,1024]{2,1,0:T(8,128)(2,1)} %all-gather.3.cloned.1.call-done) | copy-start | bytes 6291460
  60.2 1.3 copy-start.4
  92.0 3.6 %copy-start.3 = (bf16[4,256,1024]{2,1,0:T(8,128)(2,1)S(1)}, bf16[4,256,1024]{2,1,0:T(8,128)(2,1)}, u32[]{:S(2)}) copy-start(bf16[4,256,1024]{2,1,0:T(8,128)(2,1)} %all-gather.5.cloned.1.call-done) | copy-start | bytes 6291460
  92.0 3.6 %copy-start.5 = (f32[4,256,512]{2,1,0:T(8,128)S(1)}, f32[4,256,512]{2,1,0:T(8,128)}, u32[]{:S(2)}) copy-start(f32[4,256,512]{2,1,0:T(8,128)} %copy-done.4) | copy-start | bytes 6291460
  92.0 3.7 %copy-start.17 = (bf16[512,1024]{1,0:T(8,128)(2,1)S(1)}, bf16[512,1024]{1,0:T(8,128)(2,1)}, u32[]{:S(2)}) copy-start(bf16[512,1024]{1,0:T(8,128)(2,1)} %param.24) | copy-start | bytes 3145732
  95.8 2.1 copy-start.26
  97.8 2.3 copy-start.1
  97.8 2.3 copy-start.8
  102.4 2.3 copy-start.11
  107.0 134.8 %reduce-scatter.9.cloned.1.call-start = ((), (), s32[]{:S(2)}) async-start(), calls=%async_computation.5 | async-start | bytes 2621440
  107.3 2.7 copy-start.2
  107.3 2.7 copy-start.9
  107.3 2.7 copy-start.10
  112.7 167.2 %reduce-scatter.7.cloned.1.call-start = ((), (), s32[]{:S(2)}) async-start(), calls=%async_computation.4 | async-start | bytes 2621440
  112.7 2.7 copy-start.12
  112.7 2.7 copy-start.13
  203.7 2.9 %copy-start.16 = (bf16[1024,512]{1,0:T(8,128)(2,1)S(1)}, bf16[1024,512]{1,0:T(8,128)(2,1)}, u32[]{:S(2)}) copy-start(bf16[1024,512]{1,0:T(8,128)(2,1)} %get-tuple-element.11) | copy-start | bytes 3145732
  206.6 1.6 copy-start.15
  208.3 1.6 copy-start.14
  209.8 70.0 %copy-start.6 = (bf16[1,256,1024]{2,1,0:T(8,128)(2,1)S(1)}, bf16[1,256,1024]{2,1,0:T(8,128)(2,1)}, u32[]{:S(2)}) copy-start(bf16[1,256,1024]{2,1,0:T(8,128)(2,1)} %param.31) | copy-start | bytes 1572868
Sparse Core Ops, SparseCore 0:
  17.0 37.8 all-gather.2
  56.8 35.1 all-gather.4
  107.1 96.5 all-reduce.4
  206.5 35.2 reduce-scatter.8
  244.6 35.1 reduce-scatter.6
where the time goes:
time: 289 us
  waiting for transfers between devices  216 us (75%)
  matrix products  32.2 us (11%)
  other arithmetic  20.2 us (7%)
  between operations  14.2 us (5%)
  local copies, waits for them, and re-layouts  5.66 us (2%)
    psum x1, waiting for transfers between devices, body(): lax.psum(local_mean_in.astype(jnp.bfloat16), 'dp').astype(jnp.float32)  85.7 us
    unnamed x7, waiting for transfers between devices  67.8 us
    all_gather x1, waiting for transfers between devices, body(): gathered = lax.all_gather(normed, 'seq', axis=0, tiled=True)  37 us
    all_gather x1, waiting for transfers between devices, body(): cot_all = lax.all_gather(cotangent, 'seq', axis=0, tiled=True)  25.8 us
    dot_general x4, matrix products, contract_last(): lax.dot_general(left, right, (((1,), (1,)), ((), ())), preferred_element_...  11 us
    dot_general x4, matrix products, contract_first(): lax.dot_general(left, right, (((0,), (0,)), ((), ())), preferred_element_...  9.14 us
  transfers between devices with their start and end apart: 5, of which 5 were waited for; matrix products, arithmetic and copies ran while one was open for 10% of the time, Pallas kernels for 0%

commit v1 on v0

--- a/solution.py
+++ b/solution.py
@@ -103,7 +103,12 @@
         (plain + noisy * out_signs_f).astype(jnp.bfloat16), "seq", scatter_dimension=0, tiled=True
     ).astype(jnp.float32)
     block_out = (resid_f + mixed).astype(bf)
-    cot_all = lax.all_gather(cotangent, "seq", axis=0, tiled=True)
+    ring = [cotangent]
+    for hop in range(3):
+        ring.append(lax.ppermute(ring[-1], "seq", [(dev, (dev + 1) % 4) for dev in range(4)]))
+    cot_all = jnp.roll(
+        jnp.concatenate(ring[::-1], axis=0), (lax.axis_index("seq") + 1) * ring[0].shape[0], axis=0
+    )
     cot_flat = cot_all.reshape(rows, width)
     cot_flip_flat = (cot_all * out_signs).reshape(rows, width)
     dhidden = contract_last(cot_flat, mean_out).reshape(group_images, patches, hidden_local)

time: 289 us -> 283 us (0.979)
  waiting for transfers between devices: 216 us -> 201 us
  starting transfers between devices: 0.6 us -> 8.38 us
    ppermute x0 -> x3, waiting for transfers between devices: none -> 47.3 us  [body(): lax.ppermute(ring[-1], 'seq', [(dev, (dev + 1) % 4) for dev in range(4)])]
    all_gather x1, waiting for transfers between devices: 37 us -> 0.01 us  [body(): gathered = lax.all_gather(normed, 'seq', axis=0, tiled=True)]
    all_gather x1 -> x0, waiting for transfers between devices: 25.8 us -> none  [body(): cot_all = lax.all_gather(cotangent, 'seq', axis=0, tiled=True)]
    ppermute x0 -> x3, starting transfers between devices: none -> 7.99 us  [body(): lax.ppermute(ring[-1], 'seq', [(dev, (dev + 1) % 4) for dev in range(4)])]
    unnamed x57 -> x64, local copies, waits for them, and re-layouts: 4.35 us -> 7.59 us
    unnamed x7 -> x6, waiting for transfers between devices: 67.8 us -> 67.3 us
  transfers between devices with their start and end apart: 5 -> 7, of which waited for: 5 -> 6; matrix products, arithmetic and copies ran while one was open for 10% -> 9% of each run, Pallas kernels for 0% -> 0%
where the time goes in v1:
time: 283 us; the launch traced here: 282 us
  waiting for transfers between devices  201 us (71%)
  matrix products  31.3 us (11%)
  other arithmetic  20 us (7%)
  between operations  14.2 us (5%)
  starting transfers between devices  8.38 us (3%)
  local copies, waits for them, and re-layouts  7.96 us (3%)
    psum x1, waiting for transfers between devices, body(): lax.psum(local_mean_in.astype(jnp.bfloat16), 'dp').astype(jnp.float32)  86.2 us
    unnamed x6, waiting for transfers between devices  67.3 us
    ppermute x3, waiting for transfers between devices, body(): lax.ppermute(ring[-1], 'seq', [(dev, (dev + 1) % 4) for dev in range(4)])  47.3 us
    dot_general x4, matrix products, contract_last(): lax.dot_general(left, right, (((1,), (1,)), ((), ())), preferred_element_...  10 us
    dot_general x4, matrix products, contract_first(): lax.dot_general(left, right, (((0,), (0,)), ((), ())), preferred_element_...  9.16 us
    ppermute x3, starting transfers between devices, body(): lax.ppermute(ring[-1], 'seq', [(dev, (dev + 1) % 4) for dev in range(4)])  7.99 us
    unnamed x64, local copies, waits for them, and re-layouts  7.59 us
  transfers between devices with their start and end apart: 7, of which 6 were waited for; matrix products, arithmetic and copies ran while one was open for 9% of the time, Pallas kernels for 0%

profile of v1, /device:TPU:0, one launch (start us, length us, event | category | flops | bytes accessed | tf_op | source)
XLA Modules:
  0.0 282.5 jit_solution(2458096142738740568)
XLA Ops:
  7.2 0.0 all-gather.2.cloned.1.call-start
  7.2 1.4 copy.42
  8.6 1.2 copy.40
  9.9 0.2 copy.41
  10.1 0.8 multiply_reduce_fusion
  10.8 0.7 fusion
  11.6 0.9 divide_convert_fusion
  12.4 0.1 bitcast_convert_fusion.2
  12.6 0.3 copy.44
  12.9 0.2 copy-done.24
  13.2 1.3 convert_reduce_fusion
  14.5 0.3 fusion.55
  14.8 1.1 fusion.49
  15.9 0.0 all-gather.2.cloned.1.call-update
  15.9 0.0 all-reduce.5.cloned.1.call-start
  15.9 3.0 %collective-permute-start = (bf16[1,256,1024]{2,1,0:T(8,128)(2,1)S(1)}, bf16[1,256,1024]{2,1,0:T(8,128)(2,1)S(1)}, u32[]{:S(2)}, u32[]{:S(2)}) collective-permute-start(bf16[1,256,1024]{2,1,0:T(8,128)(2,1)S(1)} %copy-done.1), channel_id=1, source_target_pairs={{0,1},{1,2},{2,3},{3,0},{4,5},{5,6},{6,7},{7,4},{8,9},{9,10},{10,1... | collective-permute-start | bytes 1572872 | tf_op jit(solution)/shard_map/ppermute | solution.py:108
  19.0 15.9 %collective-permute-done = bf16[1,256,1024]{2,1,0:T(8,128)(2,1)S(1)} collective-permute-done((bf16[1,256,1024]{2,1,0:T(8,128)(2,1)S(1)}, bf16[1,256,1024]{2,1,0:T(8,128)(2,1)S(1)}, u32[]{:S(2)}, u32[]{:S(2)}) %collective-permute-start) | collective-permute-done | bytes 524320 | tf_op jit(solution)/shard_map/ppermute | solution.py:108
  34.8 2.5 collective-permute-start.1
  37.3 16.8 %collective-permute-done.1 = bf16[1,256,1024]{2,1,0:T(8,128)(2,1)S(1)} collective-permute-done((bf16[1,256,1024]{2,1,0:T(8,128)(2,1)S(1)}, bf16[1,256,1024]{2,1,0:T(8,128)(2,1)S(1)}, u32[]{:S(2)}, u32[]{:S(2)}) %collective-permute-start.1) | collective-permute-done | bytes 524320 | tf_op jit(solution)/shard_map/ppermute | solution.py:108
  54.1 2.5 collective-permute-start.2
  56.6 14.6 %collective-permute-done.2 = bf16[1,256,1024]{2,1,0:T(8,128)(2,1)} collective-permute-done((bf16[1,256,1024]{2,1,0:T(8,128)(2,1)S(1)}, bf16[1,256,1024]{2,1,0:T(8,128)(2,1)}, u32[]{:S(2)}, u32[]{:S(2)}) %collective-permute-start.2) | collective-permute-done | bytes 524320 | tf_op jit(solution)/shard_map/ppermute | solution.py:108
  71.3 1.1 constant_dynamic-update-slice_fusion.7
  72.5 1.2 constant_dynamic-update-slice_fusion.3
  73.9 1.9 copy-done.18
  75.8 2.6 fusion.27
  78.5 3.3 %fusion.31 = f32[4,256,512]{2,1,0:T(8,128)S(1)} fusion(bf16[4,256,1024]{2,1,0:T(8,128)(2,1)} %all-gather.2.cloned.1.call-done, bf16[4,1024]{1,0:T(4,128)(2,1)S(1)} %get-tuple-element.19, bf16[1024,512]{1,0:T(8,128)(2,1)S(1)} %copy-done.4, bf16[1024,512]{1,0:T(8,128)(2,1)} %param.22), kind=kOutput, calls=%fused_computation.55 | convolution fusion | flops 1076887552 | bytes 6299648 | tf_op jit(solution)/shard_map/dot_general | solution.py:89
  81.8 1.9 fusion.81
  83.7 4.8 %fusion.8 = bf16[4,256,512]{2,1,0:T(8,128)(2,1)S(1)} fusion(f32[4,256,512]{2,1,0:T(8,128)S(1)} %get-tuple-element.28, u8[256,512]{1,0:T(8,128)(4,1)S(1)} %get-tuple-element.7, u8[256,512]{1,0:T(8,128)(4,1)S(1)} %get-tuple-element.6), kind=kLoop, calls=%fused_computation.18 | loop fusion | flops 36700160 | bytes 3407872 | tf_op jit(solution)/shard_map/convert_element_type | solution.py:95
  88.5 2.3 bitcast_convert_fusion
  90.8 2.4 fusion.5
  93.2 2.1 fusion.14
  95.3 2.3 bitcast_convert_fusion.1
  97.5 2.3 fusion.3
  99.8 0.3 reduce-scatter.9.cloned.1.call-start
  100.1 2.7 fusion.62
  102.8 2.6 add_convert_fusion
  105.5 0.0 reduce-scatter.7.cloned.1.call-start
  105.6 2.7 fusion.60
  108.3 2.6 add_convert_fusion.1
  110.9 86.2 %all-reduce.5.cloned.1.call-done = (bf16[1024,512]{1,0:T(8,128)(2,1)}, bf16[1024,512]{1,0:T(8,128)(2,1)}, bf16[512,1024]{1,0:T(8,128)(2,1)}, bf16[512,1024]{1,0:T(8,128)(2,1)}) async-done(((bf16[1024,512]{1,0:T(8,128)(2,1)}, bf16[1024,512]{1,0:T(8,128)(2,1)}, bf16[512,1024]{1,0:T(8,128)(2,1)}, bf16[512,1024]{1,0:T(8,128)(2,1)}), (bf16[1024,512]{1,0:T(8,128)(2,1)}, bf16[1024,512]{1,0:T(8,128)(2,1)}, ...) | async-done | bytes 4194320 | tf_op jit(solution)/shard_map/psum | solution.py:145
  197.0 2.9 %convert_element_type.173 = f32[1024,512]{1,0:T(8,128)} convert(bf16[1024,512]{1,0:T(8,128)(2,1)} %get-tuple-element.10) | non-fusion elementwise | flops 524288 | bytes 3145728 | tf_op jit(solution)/shard_map/convert_element_type | solution.py:145
  200.0 1.6 convert_element_type.175
  201.6 1.6 convert_element_type.177
  203.2 1.6 convert_element_type.179
  204.7 30.6 %reduce-scatter.9.cloned.1.call-done = bf16[1,256,1024]{2,1,0:T(8,128)(2,1)} async-done(((bf16[4,256,1024]{2,1,0:T(8,128)(2,1)}), bf16[1,256,1024]{2,1,0:T(8,128)(2,1)}) %reduce-scatter.9.cloned.1.call-update) | async-done | bytes 524304
  235.3 1.4 fusion.65
  236.7 36.6 %reduce-scatter.7.cloned.1.call-done = bf16[1,256,1024]{2,1,0:T(8,128)(2,1)} async-done(((bf16[4,256,1024]{2,1,0:T(8,128)(2,1)}), bf16[1,256,1024]{2,1,0:T(8,128)(2,1)}) %reduce-scatter.7.cloned.1.call-update) | async-done | bytes 524304
  273.4 2.6 fusion.54
  (70 shorter events, 0.5 us)
Async XLA Ops:
  7.2 74.6 %copy-start = (bf16[1024,512]{1,0:T(8,128)(2,1)S(1)}, bf16[1024,512]{1,0:T(8,128)(2,1)}, u32[]{:S(2)}) copy-start(bf16[1024,512]{1,0:T(8,128)(2,1)} %param.21) | copy-start | bytes 3145732
  7.2 2.7 copy-start.17
  7.2 71.3 %all-gather.2.cloned.1.call-start = ((), (), s32[]{:S(2)}) async-start(), calls=%async_computation.2 | async-start | bytes 2621440 | tf_op jit(solution)/shard_map/all_gather | solution.py:83
  12.4 0.7 copy-start.24
  13.1 2.8 copy-start.1
  13.1 24.2 %copy-start.22 = (s32[4,512]{1,0:T(4,128)S(1)}, s32[4,512]{1,0:T(4,128)}, u32[]{:S(2)}) copy-start(s32[4,512]{1,0:T(4,128)} %param.28) | copy-start | bytes 24580
  13.1 43.5 %copy-start.23 = (s32[4,512]{1,0:T(4,128)S(1)}, s32[4,512]{1,0:T(4,128)}, u32[]{:S(2)}) copy-start(s32[4,512]{1,0:T(4,128)} %param.29) | copy-start | bytes 24580
  13.1 43.5 %copy-start.20 = (s32[4,1024]{1,0:T(4,128)S(1)}, s32[4,1024]{1,0:T(4,128)}, u32[]{:S(2)}) copy-start(s32[4,1024]{1,0:T(4,128)} %param.27) | copy-start | bytes 49156
  13.2 43.5 %copy-start.21 = (s32[4,1024]{1,0:T(4,128)S(1)}, s32[4,1024]{1,0:T(4,128)}, u32[]{:S(2)}) copy-start(s32[4,1024]{1,0:T(4,128)} %param.30) | copy-start | bytes 49156
  15.9 181.2 %all-reduce.5.cloned.1.call-start = ((), (), s32[]{:S(2)}) async-start(), calls=%async_computation.5 | async-start | bytes 8388608 | tf_op jit(solution)/shard_map/psum | solution.py:145
  15.9 18.9 %collective-permute-start = (bf16[1,256,1024]{2,1,0:T(8,128)(2,1)S(1)}, bf16[1,256,1024]{2,1,0:T(8,128)(2,1)S(1)}, u32[]{:S(2)}, u32[]{:S(2)}) collective-permute-start(bf16[1,256,1024]{2,1,0:T(8,128)(2,1)S(1)} %copy-done.1), channel_id=1, source_target_pairs={{0,1},{1,2},{2,3},{3,0},{4,5},{5,6},{6,7},{7,4},{8,9},{9,10},{10,1... | collective-permute-start | bytes 1572872 | tf_op jit(solution)/shard_map/ppermute | solution.py:108
  34.8 19.3 %collective-permute-start.1 = (bf16[1,256,1024]{2,1,0:T(8,128)(2,1)S(1)}, bf16[1,256,1024]{2,1,0:T(8,128)(2,1)S(1)}, u32[]{:S(2)}, u32[]{:S(2)}) collective-permute-start(bf16[1,256,1024]{2,1,0:T(8,128)(2,1)S(1)} %collective-permute-done), channel_id=1, source_target_pairs={{0,1},{1,2},{2,3},{3,0},{4,5},{5,6},{6,7},{7,4},{8,9},{9,10},{10,1... | collective-permute-start | bytes 1572872 | tf_op jit(solution)/shard_map/ppermute | solution.py:108
  54.1 17.2 %collective-permute-start.2 = (bf16[1,256,1024]{2,1,0:T(8,128)(2,1)S(1)}, bf16[1,256,1024]{2,1,0:T(8,128)(2,1)}, u32[]{:S(2)}, u32[]{:S(2)}) collective-permute-start(bf16[1,256,1024]{2,1,0:T(8,128)(2,1)S(1)} %collective-permute-done.1), channel_id=1, source_target_pairs={{0,1},{1,2},{2,3},{3,0},{4,5},{5,6},{6,7},{7,4},{8,9},{9,10},{10,1... | collective-permute-start | bytes 1572872 | tf_op jit(solution)/shard_map/ppermute | solution.py:108
  72.5 3.3 %copy-start.8 = (bf16[512,1024]{1,0:T(8,128)(2,1)S(1)}, bf16[512,1024]{1,0:T(8,128)(2,1)}, u32[]{:S(2)}) copy-start(bf16[512,1024]{1,0:T(8,128)(2,1)} %param.26) | copy-start | bytes 3145732
  72.5 3.3 %copy-start.11 = (bf16[512,1024]{1,0:T(8,128)(2,1)S(1)}, bf16[512,1024]{1,0:T(8,128)(2,1)}, u32[]{:S(2)}) copy-start(bf16[512,1024]{1,0:T(8,128)(2,1)} %param.25) | copy-start | bytes 3145732
  73.9 1.9 copy-start.18
  75.8 2.6 copy-start.4
  78.5 3.3 %copy-start.25 = (bf16[4,256,1024]{2,1,0:T(8,128)(2,1)S(1)}, bf16[4,256,1024]{2,1,0:T(8,128)(2,1)}, u32[]{:S(2)}) copy-start(bf16[4,256,1024]{2,1,0:T(8,128)(2,1)} %all-gather.2.cloned.1.call-done) | copy-start | bytes 6291460
  81.8 6.7 %copy-start.19 = (bf16[8,256,1024]{2,1,0:T(8,128)(2,1)S(1)}, bf16[8,256,1024]{2,1,0:T(8,128)(2,1)}, u32[]{:S(2)}) copy-start(bf16[8,256,1024]{2,1,0:T(8,128)(2,1)} %copy-done.18) | copy-start | bytes 12582916
  88.5 2.3 copy-start.9
  90.8 2.4 copy-start.16
  90.8 2.4 copy-start.26
  95.3 2.3 copy-start.2
  95.3 2.3 copy-start.5
  99.8 135.5 %reduce-scatter.9.cloned.1.call-start = ((), (), s32[]{:S(2)}) async-start(), calls=%async_computation.4 | async-start | bytes 2621440
  100.1 2.7 copy-start.3
  100.1 2.7 copy-start.6
  100.1 2.7 copy-start.7
  105.5 167.9 %reduce-scatter.7.cloned.1.call-start = ((), (), s32[]{:S(2)}) async-start(), calls=%async_computation.3 | async-start | bytes 2621440
  105.5 2.7 copy-start.10
  105.5 2.7 copy-start.12
  197.0 2.9 %copy-start.15 = (bf16[1024,512]{1,0:T(8,128)(2,1)S(1)}, bf16[1024,512]{1,0:T(8,128)(2,1)}, u32[]{:S(2)}) copy-start(bf16[1024,512]{1,0:T(8,128)(2,1)} %get-tuple-element.11) | copy-start | bytes 3145732
  200.0 1.6 copy-start.14
  201.6 1.6 copy-start.13
Sparse Core Ops, SparseCore 0:
  16.0 50.9 all-gather.1
  99.9 97.0 all-reduce.4
  200.0 35.2 reduce-scatter.8
  238.1 35.1 reduce-scatter.6
